TPU v7x, 1024 devices: a whole 4x4x32 slice. The times are simulated.
1024 devices in a mesh: gx: 128 (over x, z), gy: 8 (over y, core).
Axes of the slice: x: 4, y: 4, z: 32, core: 2. Of those that a mesh axis runs over, the one named last changes fastest.
Arguments:
- state: float32 [2097152, 128], P(('gx', 'gy')), may hold values from 0 to 1
- velocity: bfloat16 [3, 3, 2048, 128, 128], P(None, None, 'gx', 'gy'), may hold values from -3 to 3
- cells: int32 [3, 3, 2097152], P(None, None, ('gx', 'gy')), may hold values from -1 to 126, as said below
- slots: int32 [3, 2097152], P(None, ('gx', 'gy')), may hold values from 0 to 2047, as said below
- counts: int32 [3, 128, 8, 8], P(None, 'gx', 'gy'), may hold values from 0 to 64, as said below
Outputs:
- final_state: float32 [2097152, 128], P(('gx', 'gy'))
Inputs may be any that keep to these rules, and one draw needn't show every extreme that they name: For every section and device the 2048 values of slots are a permutation of 0 to 2047. counts[s, i, j, r] equals counts[s, i', j', r xor 1] where (i', j') is the neighbour of (i, j) in direction r; some device sends exactly 64 in every section. cells[s, 0] lies in -1 to 15, cells[s, 1] in -1 to 15, cells[s, 2] in 0 to 126.
All inputs are finite; a program needn't handle non-finite values.
Results may differ from a plain program's by a relative error of at most 0.0003.
Values may be sent and summed in bfloat16 or wider, within the bound.
A program may use at most 32 MiB of HBM per device.

v0:
```python
import jax
import jax.numpy as jnp
from jax import lax
from jax.experimental import pallas as pl
from jax.experimental.pallas import tpu as pltpu
from jax.sharding import PartitionSpec as P

GAMMA = (8.0 / 15.0, 5.0 / 12.0, 3.0 / 4.0)
ZETA = (0.0, -17.0 / 60.0, -5.0 / 12.0)
OFFSETS = ((1, 0), (-1, 0), (0, 1), (0, -1), (1, 1), (-1, -1), (1, -1), (-1, 1))
CAP = 64
SLOTS = 2048
MOVE = 512
CHUNK = 512
F32 = jnp.float32
BF16 = jnp.bfloat16
I32 = jnp.int32
VMEM = pltpu.VMEM
SMEM = pltpu.SMEM
ANY = pl.ANY


def iota(shape, dim):
    return lax.broadcasted_iota(I32, shape, dim)


def lane_gather(x, index):
    return jnp.take_along_axis(x, index, axis=1, mode="promise_in_bounds")


def copy_rows(target, source, index, shift=0):
    def body(i, carry):
        for u in range(16):
            k = i * 16 + u
            target[pl.ds(k, 1), :] = source[pl.ds(index(k), 1), :]
        return carry

    lax.fori_loop(0, MOVE // 16, body, 0)


def prep_kernel(counts, leaving, slots, state, vel, pv, inv, ptr, dst, faces, corners, rows0, planes):
    for b in range(16):
        pv[:, b * 128 : (b + 1) * 128] = state[b * 128 : (b + 1) * 128, :].T[0:8, :]
    for j in range(9):
        planes[...] = vel[j * 256 : (j + 1) * 256, :].astype(F32)
        for side, y in ((0, 0), (1, 15)):
            faces[side, j] = planes[pl.ds(y, 16, stride=16), :].astype(BF16)
    for c in range(4):
        x, y = 15 * (c // 2), 15 * (c % 2)
        picked = [vel[j * 256 + x * 16 : j * 256 + x * 16 + 16, :].astype(F32)[y : y + 1, :] for j in range(9)]
        picked.append(jnp.zeros((7, 128), F32))
        corners[c] = jnp.concatenate(picked, axis=0).astype(BF16)
    loc = iota((16, 128), 0) * 128 + iota((16, 128), 1)
    lane = iota((1, 128), 1)
    row = iota((16, 128), 0)
    for s in range(3):
        heads = []
        tails = []
        for g in range(4):
            q = slots[s : s + 1, g * 128 : (g + 1) * 128]
            limit = jnp.where(lane < CAP, counts[s, 2 * g], counts[s, 2 * g + 1])
            valid = jnp.where(lane < CAP, lane, lane - CAP) < limit
            dst[s, g : g + 1, :] = jnp.where(valid, q, SLOTS)
            low = jnp.broadcast_to(q & 127, (8, 128))
            mine = jnp.broadcast_to(q >> 7, (16, 128)) == row
            found = jnp.concatenate([lane_gather(loc[0:8], low), lane_gather(loc[8:16], low)], axis=0)
            ptr[s, g : g + 1, :] = jnp.sum(jnp.where(mine, found, 0), axis=0, keepdims=True)
            place = (lane + g * 128) ^ CAP
            chosen = jnp.where(mine, jnp.where(valid, 1.0, 0.0), 0.0)
            upper = (place >> 5).astype(F32)
            lower = (place & 31).astype(F32)
            heads.append(jnp.concatenate([chosen, chosen * upper, chosen * lower], axis=0))
            tails.append(jnp.where(iota((128, 128), 0) == (q & 127), 1.0, 0.0))
        head = jnp.concatenate(heads, axis=1).astype(BF16)
        tail = jnp.concatenate(tails, axis=1).astype(BF16)
        table = lax.dot_general(head, tail, (((1,), (1,)), ((), ())), preferred_element_type=F32)
        value = (table[16:32] * 32.0 + table[32:48]).astype(I32)
        hit = table[0:16] > 0.5
        inv[s] = jnp.where(hit, value, -1)
        loc = jnp.where(hit, SLOTS + s * MOVE + (value ^ CAP), loc)
    copy_rows(rows0, state, lambda k: leaving[0, k])


def split(x):
    high = x.astype(BF16).astype(F32)
    return high, x - high


def step_kernel(
    ptr, pv0, inv, cells, slots, faces, corners, rows0, state, vel,
    pv_out, rows_out,
    pool, rows, landed, block, grid_v, halo_x, halo_y, halo_c, field, wx_table, sums, pv, out_pv, in_pv,
    local_sem, x_send, x_recv, y_send, y_recv, c_send, c_recv, r_send, r_recv, p_send, p_recv,
):
    me_x, me_y = lax.axis_index("gx"), lax.axis_index("gy")
    n_x, n_y = lax.axis_size("gx"), lax.axis_size("gy")

    def toward(r):
        dx, dy = OFFSETS[r]
        return (lax.rem(me_x + dx + n_x, n_x), lax.rem(me_y + dy + n_y, n_y))

    def remote(source, target, send, recv, r):
        return pltpu.make_async_remote_copy(
            src_ref=source, dst_ref=target, send_sem=send, recv_sem=recv,
            device_id=toward(r), device_id_type=pl.DeviceIdType.MESH,
        )

    load_vel = pltpu.make_async_copy(vel, block, local_sem.at[0])
    load_vel.start()
    load_state = pltpu.make_async_copy(state, pool.at[pl.ds(0, SLOTS)], local_sem.at[1])
    load_state.start()

    barrier = pltpu.get_barrier_semaphore()
    for r in range(8):
        pl.semaphore_signal(barrier, inc=1, device_id=toward(r), device_id_type=pl.DeviceIdType.MESH)
    pv[...] = pv0[...]
    load_vel.wait()
    for s in range(3):
        for k in range(3):
            own = block[s * 3 + k].reshape(256, 128)
            field[s, k * 256 : (k + 1) * 256, 0:128] = own
            field[s, k * 256 : (k + 1) * 256, 128:256] = own
    pl.semaphore_wait(barrier, 8)

    def rows_target(s, r):
        back = r ^ 1
        if s == 0:
            return pool.at[pl.ds(SLOTS + back * CAP, CAP)]
        return landed.at[s - 1, pl.ds(back * CAP, CAP)]

    def halo(s):
        part = pl.ds(s * 3, 3)
        copies = []
        for side, x, r in ((1, 0, 1), (0, 15, 0)):
            copies.append(remote(block.at[part, x], halo_x.at[side, part], x_send.at[s, side], x_recv.at[s, side], r))
        for side, edge, r in ((1, 0, 3), (0, 1, 2)):
            copies.append(remote(faces.at[edge, part], halo_y.at[side, part], y_send.at[s, side], y_recv.at[s, side], r))
        return copies

    corner_copies = [
        remote(corners.at[c], halo_c.at[3 - c], c_send.at[c], c_recv.at[3 - c], r)
        for c, r in ((0, 5), (1, 7), (2, 6), (3, 4))
    ]
    halos = [halo(s) for s in range(3)]
    row_copies = [
        [
            remote((rows0 if s == 0 else rows.at[s - 1]).at[pl.ds(r * CAP, CAP)], rows_target(s, r), r_send.at[s, r], r_recv.at[s, r ^ 1], r)
            for r in range(8)
        ]
        for s in range(3)
    ]
    pv_copies = [
        [remote(out_pv.at[s, r // 2], in_pv.at[s, r ^ 1], p_send.at[s, r], p_recv.at[s, r ^ 1], r) for r in range(8)]
        for s in range(3)
    ]
    for copy in halos[0] + corner_copies:
        copy.start()
    for copy in row_copies[0]:
        copy.start()
    for copy in halos[1] + halos[2]:
        copy.start()

    def both(target, value):
        target[:, 0:128] = value
        target[:, 128:256] = value

    def place_halo(s):
        for copy in halos[s]:
            copy.wait_recv()
        for side in range(2):
            both(field.at[s, pl.ds(768 + side * 48, 48)], halo_x[side, s * 3 : s * 3 + 3].reshape(48, 128))
            both(field.at[s, pl.ds(864 + side * 48, 48)], halo_y[side, s * 3 : s * 3 + 3].reshape(48, 128))
        for c in range(4):
            both(field.at[s, pl.ds(960 + c * 16, 16)], halo_c[c])

    def interpolate(s):
        def chunk(i, carry):
            at = pl.ds(pl.multiple_of(i * CHUNK, CHUNK), CHUNK)
            fx, fy, fz = pv[0:1, at], pv[1:2, at], pv[2:3, at]
            cx, cy, cz = cells[s, 0:1, at], cells[s, 1:2, at], cells[s, 2:3, at]
            near_hi, near_lo = split(1.0 - fz)
            far_hi, far_lo = split(fz)
            level = iota((128, CHUNK), 0)
            near = level == cz
            far = level == cz + 1
            weight = jnp.concatenate(
                [
                    jnp.where(near, near_hi, jnp.where(far, far_hi, 0.0)).astype(BF16),
                    jnp.where(near, near_lo, jnp.where(far, far_lo, 0.0)).astype(BF16),
                ],
                axis=0,
            )
            sums[...] = jnp.dot(field[s], weight, preferred_element_type=F32)
            spot = iota((16, CHUNK), 0)
            wx = jnp.where(spot == cx, 1.0 - fx, jnp.where(spot == cx + 1, fx, 0.0))
            wy = jnp.where(spot == cy, 1.0 - fy, jnp.where(spot == cy + 1, fy, 0.0))
            wx_table[...] = wx
            wx_low = jnp.where(cx == -1, 1.0 - fx, 0.0)
            wx_high = jnp.where(cx == 15, fx, 0.0)
            wy_low = jnp.where(cy == -1, 1.0 - fy, 0.0)
            wy_high = jnp.where(cy == 15, fy, 0.0)
            corner = jnp.zeros((16, CHUNK), F32)
            for c, w in enumerate((wx_low * wy_low, wx_low * wy_high, wx_high * wy_low, wx_high * wy_high)):
                corner = corner + sums[960 + c * 16 : 976 + c * 16, :] * w
            old = pv[:, at]
            new = []
            speeds = []
            for k in range(3):
                along = sums[768 + k * 16 : 784 + k * 16, :] * wx_low + sums[816 + k * 16 : 832 + k * 16, :] * wx_high
                for x in range(16):
                    along = along + sums[k * 256 + x * 16 : k * 256 + x * 16 + 16, :] * wx_table[x : x + 1, :]
                edge = sums[864 + k * 16 : 880 + k * 16, :] * wy_low + sums[912 + k * 16 : 928 + k * 16, :] * wy_high
                total = along * wy + edge * wx + jnp.where(spot == s * 3 + k, corner, 0.0)
                speed = jnp.sum(total, axis=0, keepdims=True)
                speeds.append(speed)
                new.append(old[k : k + 1] + GAMMA[s] * speed + ZETA[s] * old[3 + k : 4 + k])
            for k in range(3):
                pv[k : k + 1, at] = new[k]
                pv[3 + k : 4 + k, at] = speeds[k]
            return carry

        lax.fori_loop(0, SLOTS // CHUNK, chunk, 0)

    def collect(s):
        for g in range(4):
            q = slots[s : s + 1, g * 128 : (g + 1) * 128]
            low = jnp.broadcast_to(q & 127, (8, 128))
            high = jnp.broadcast_to(q >> 7, (8, 128))
            picked = jnp.zeros((8, 128), F32)
            for h in range(16):
                picked = jnp.where(high == h, lane_gather(pv[:, h * 128 : (h + 1) * 128], low), picked)
            out_pv[s, g] = picked

    def deliver(s):
        lane = iota((8, 128), 1)
        came = [jnp.where(lane < CAP, in_pv[s, 2 * g + 1], in_pv[s, 2 * g]) for g in range(4)]
        for h in range(16):
            at = slice(h * 128, (h + 1) * 128)
            source = jnp.broadcast_to(inv[s, h : h + 1, :], (8, 128))
            low = source & 127
            high = source >> 7
            value = pv[:, at]
            for g in range(4):
                value = jnp.where(high == g, lane_gather(came[g], low), value)
            pv[:, at] = value

    for copy in corner_copies:
        copy.wait_recv()
    for s in range(3):
        place_halo(s)
        interpolate(s)
        collect(s)
        for copy in pv_copies[s]:
            copy.start()
        if s == 0:
            load_state.wait()
        for copy in row_copies[s]:
            copy.wait_recv()
        if s == 1:
            pool[SLOTS + MOVE : SLOTS + 2 * MOVE, :] = landed[0]
        if s < 2:
            copy_rows(rows.at[s], pool, lambda k: ptr[s + 1, k])
            for copy in row_copies[s + 1]:
                copy.start()
        else:
            out_a = pltpu.make_async_copy(pool.at[pl.ds(SLOTS, 2 * MOVE)], rows_out.at[pl.ds(0, 2 * MOVE)], local_sem.at[2])
            out_a.start()
            out_b = pltpu.make_async_copy(landed.at[1], rows_out.at[pl.ds(2 * MOVE, MOVE)], local_sem.at[3])
            out_b.start()
        for copy in pv_copies[s]:
            copy.wait_recv()
        deliver(s)
    pv_out[...] = pv[...]
    out_a.wait()
    out_b.wait()
    for copies in halos + [corner_copies] + row_copies + pv_copies:
        for copy in copies:
            copy.wait_send()


def finish_kernel(dst, state, rows, pv, out, held, sem):
    load = pltpu.make_async_copy(state, held.at[pl.ds(0, SLOTS)], sem)
    load.start()
    load.wait()
    for s in range(3):
        def body(i, carry):
            for u in range(16):
                k = i * 16 + u
                held[pl.ds(dst[s, k], 1), :] = rows[pl.ds(s * MOVE + k, 1), :]
            return carry

        lax.fori_loop(0, MOVE // 16, body, 0)
    for b in range(16):
        held[b * 128 : (b + 1) * 128, 0:8] = pv[:, b * 128 : (b + 1) * 128].T
    store = pltpu.make_async_copy(held.at[pl.ds(0, SLOTS)], out, sem)
    store.start()
    store.wait()


def whole(space):
    return pl.BlockSpec(memory_space=space)


def shape(dims, dtype):
    return jax.ShapeDtypeStruct(dims, dtype)


def local(state, velocity, cells, slots, counts):
    flat = velocity.reshape(2304, 128)
    pv, inv, ptr, dst, faces, corners, rows0 = pl.pallas_call(
        prep_kernel,
        grid=(1,),
        out_shape=(
            shape((8, SLOTS), F32), shape((3, 16, 128), I32), shape((3, 4, 128), I32), shape((3, 4, 128), I32),
            shape((2, 9, 16, 128), BF16), shape((4, 16, 128), BF16), shape((MOVE, 128), F32),
        ),
        in_specs=[
            whole(SMEM),
            pl.BlockSpec((3, MOVE), lambda i: (0, 0), memory_space=SMEM),
            pl.BlockSpec((3, MOVE), lambda i: (0, 0)),
            whole(VMEM),
            whole(VMEM),
        ],
        out_specs=[whole(VMEM)] * 7,
        scratch_shapes=[VMEM((256, 128), F32)],
        name="prep",
    )(counts.reshape(3, 8), slots, slots, state, flat)

    dma = pltpu.SemaphoreType.DMA
    pv, rows = pl.pallas_call(
        step_kernel,
        out_shape=(shape((8, SLOTS), F32), shape((3 * MOVE, 128), F32)),
        in_specs=[whole(SMEM)] + [whole(VMEM)] * 7 + [whole(ANY)] * 2,
        out_specs=[whole(VMEM), whole(ANY)],
        scratch_shapes=[
            VMEM((SLOTS + 2 * MOVE, 128), F32),
            VMEM((2, MOVE, 128), F32),
            VMEM((2, MOVE, 128), F32),
            VMEM((9, 16, 16, 128), BF16),
            VMEM((8, 128), F32),
            VMEM((2, 9, 16, 128), BF16),
            VMEM((2, 9, 16, 128), BF16),
            VMEM((4, 16, 128), BF16),
            VMEM((3, 1024, 256), BF16),
            VMEM((16, CHUNK), F32),
            VMEM((1024, CHUNK), F32),
            VMEM((8, SLOTS), F32),
            VMEM((3, 4, 8, 128), F32),
            VMEM((3, 8, 8, 128), F32),
            dma((4,)),
            dma((3, 2)), dma((3, 2)), dma((3, 2)), dma((3, 2)),
            dma((4,)), dma((4,)),
            dma((3, 8)), dma((3, 8)), dma((3, 8)), dma((3, 8)),
        ],
        compiler_params=pltpu.CompilerParams(collective_id=0, has_side_effects=True),
        name="step",
    )(ptr.reshape(3, MOVE), pv, inv, cells, slots, faces, corners, rows0, state, velocity.reshape(9, 16, 16, 128))

    return pl.pallas_call(
        finish_kernel,
        out_shape=shape((SLOTS, 128), F32),
        in_specs=[whole(SMEM), whole(ANY), whole(VMEM), whole(VMEM)],
        out_specs=whole(ANY),
        scratch_shapes=[VMEM((SLOTS + 8, 128), F32), dma],
        name="finish",
    )(dst.reshape(3, MOVE), state, rows, pv)


def solution(mesh):
    return jax.shard_map(
        local,
        mesh=mesh,
        in_specs=(
            P(("gx", "gy"), None),
            P(None, None, "gx", "gy", None),
            P(None, None, ("gx", "gy")),
            P(None, ("gx", "gy")),
            P(None, "gx", "gy", None),
        ),
        out_specs=P(("gx", "gy"), None),
        check_vma=False,
    )
```

profile of v0, /device:TPU:1, one launch (start us, length us, event | category | flops | bytes accessed | tf_op | source)
XLA Modules:
  0.0 68.0 jit_solution(4353524453375311231)
XLA Ops:
  0.0 0.0 copy-start.2
  0.0 0.7 copy-done.2
  0.7 0.6 copy.14
  1.3 3.8 %prep.1 = (f32[8,2048]{1,0:T(8,128)}, s32[3,16,128]{2,1,0:T(8,128)}, s32[3,4,128]{2,1,0:T(4,128)}, s32[3,4,128]{2,1,0:T(4,128)}, bf16[2,9,16,128]{3,2,1,0:T(8,12...) custom-call(s32[3,8]{1,0:T(4,128)} %bitcast.17, s32[3,2048]{1,0:T(4,128)} %slots.3, s32[3,2048]{1,0:T(4,128)} %slots.3, ...), custom_call_target="tpu_custom_call" | custom-call | tf_op jit(solution)/shard_map/prep/pallas_call | solution.py:310
  5.0 0.0 copy-start.1
  5.1 0.7 %copy-done.1 = s32[3,4,128]{2,1,0:T(4,128)S(1)} copy-done((s32[3,4,128]{2,1,0:T(4,128)S(1)}, s32[3,4,128]{2,1,0:T(4,128)}, u32[]{:S(2)}) %copy-start.1) | copy-done | bytes 6168
  5.7 0.0 copy-start
  5.7 0.6 copy.12
  6.3 0.1 copy-done
  6.4 0.6 copy.13
  7.0 53.7 %step.1 = (f32[8,2048]{1,0:T(8,128)}, f32[1536,128]{1,0:T(8,128)}) custom-call(s32[3,512]{1,0:T(4,128)} %bitcast.16, f32[8,2048]{1,0:T(8,128)} %get-tuple-element.16.pv0, s32[3,16,128]{2,1,0:T(8,128)} %get-tuple-element.17.inv, s32[3,3,2048]{2,1,0:T(4,128)} %cells.1, s32[3,2048]{1,0:T(4,128)} %slots.3, bf16[2,9,16,128]{3,2,1,0:T(8,128)(2,1)} %get-tuple-element.18.faces, ...), custom_call_target="tpu_custom_call" | custom-call | tf_op jit(solution)/shard_map/step/pallas_call | solution.py:330
  60.8 7.2 %finish.1 = f32[2048,128]{1,0:T(8,128)} custom-call(s32[3,512]{1,0:T(4,128)} %bitcast.15, f32[2048,128]{1,0:T(8,128)} %state.5, f32[1536,128]{1,0:T(8,128)} %get-tuple-element.21.rows, f32[8,2048]{1,0:T(8,128)} %get-tuple-element.22.pv), custom_call_target="tpu_custom_call" | custom-call | tf_op jit(solution)/shard_map/finish/pallas_call | solution.py:359
Async XLA Ops:
  0.0 0.7 %copy-start.2 = (s32[3,1,1,8]{3,2,1,0:T(1,128)S(1)}, s32[3,1,1,8]{3,2,1,0:T(1,128)}, u32[]{:S(2)}) copy-start(s32[3,1,1,8]{3,2,1,0:T(1,128)} %param.9) | copy-start | bytes 292
  5.0 0.7 %copy-start.1 = (s32[3,4,128]{2,1,0:T(4,128)S(1)}, s32[3,4,128]{2,1,0:T(4,128)}, u32[]{:S(2)}) copy-start(s32[3,4,128]{2,1,0:T(4,128)} %get-tuple-element.15) | copy-start | bytes 18436
  5.7 0.7 %copy-start = (s32[3,4,128]{2,1,0:T(4,128)S(1)}, s32[3,4,128]{2,1,0:T(4,128)}, u32[]{:S(2)}) copy-start(s32[3,4,128]{2,1,0:T(4,128)} %get-tuple-element.14) | copy-start | bytes 18436
where the time goes:
time: 68.3 us; the launch traced here: 68 us
  Pallas kernels  64.7 us (95%)
  local copies, waits for them, and re-layouts  3.25 us (5%)
    pallas_call x1, Pallas kernels, local(): pl.pallas_call(step_kernel, out_shape=(shape((8, SLOTS), F32), shape((3 *...  53.7 us
    pallas_call x1, Pallas kernels, local(): pl.pallas_call(finish_kernel, out_shape=shape((SLOTS, 128), F32), in_spec...  7.19 us
    pallas_call x1, Pallas kernels, local(): pl.pallas_call(prep_kernel, grid=(1,), out_shape=(shape((8, SLOTS), F32),...  3.78 us
    unnamed x9, local copies, waits for them, and re-layouts  3.25 us

commit v1 on v0

v1 whole, which is shorter than its diff:
```python
import jax
import jax.numpy as jnp
from jax import lax
from jax.experimental import pallas as pl
from jax.experimental.pallas import tpu as pltpu
from jax.sharding import PartitionSpec as P

GAMMA = (8.0 / 15.0, 5.0 / 12.0, 3.0 / 4.0)
ZETA = (0.0, -17.0 / 60.0, -5.0 / 12.0)
OFFSETS = ((1, 0), (-1, 0), (0, 1), (0, -1), (1, 1), (-1, -1), (1, -1), (-1, 1))
CAP = 64
SLOTS = 2048
MOVE = 512
CHUNK = 512
F32 = jnp.float32
BF16 = jnp.bfloat16
I32 = jnp.int32
VMEM = pltpu.VMEM
SMEM = pltpu.SMEM
ANY = pl.ANY


def iota(shape, dim):
    return lax.broadcasted_iota(I32, shape, dim)


def lane_gather(x, index):
    return jnp.take_along_axis(x, index, axis=1, mode="promise_in_bounds")


def copy_rows(target, source, index):
    def body(g, carry):
        for u in range(128):
            target[pl.ds(g * 128 + u, 1), :] = source[pl.ds(index(g, u), 1), :]
        return carry

    lax.fori_loop(0, MOVE // 128, body, 0)


def edges(block, y):
    picked = [block[j, x].astype(F32)[y : y + 1, :] for j in range(9) for x in range(16)]
    return jnp.concatenate(picked, axis=0).astype(BF16).reshape(9, 16, 128)


def corner_rows(block, c):
    x, y = 15 * (c // 2), 15 * (c % 2)
    picked = [block[j, x].astype(F32)[y : y + 1, :] for j in range(9)]
    picked.append(jnp.zeros((7, 128), F32))
    return jnp.concatenate(picked, axis=0).astype(BF16)


def rows_dot(a, b):
    return lax.dot_general(a, b, (((1,), (1,)), ((), ())), preferred_element_type=F32)


def tables(counts, slots, ptr, dst, home, tail, filled):
    lane = iota((1, 128), 1)
    across = iota((8, 128), 1)
    down = iota((8, 128), 0)
    leaving = [[slots[s : s + 1, g * 128 : (g + 1) * 128] for g in range(4)] for s in range(3)]
    found = {}
    for s in range(3):
        for g in range(4):
            q = leaving[s][g]
            limit = jnp.where(lane < CAP, counts[s, 0, 0, 2 * g], counts[s, 0, 0, 2 * g + 1])
            valid = jnp.where(lane < CAP, lane, lane - CAP) < limit
            dst[s * 4 + g : s * 4 + g + 1, :] = jnp.where(valid, q, SLOTS)
            code = jnp.broadcast_to(jnp.where(valid, q, -1), (8, 128))
            swapped = lane_gather(code, across ^ CAP)[0:1, :]
            at = slice(g * 128, (g + 1) * 128)
            home[s : s + 1, at] = swapped >> 7
            tail[s, :, at] = jnp.where(iota((128, 128), 0) == (swapped & 127), 1.0, 0.0).astype(BF16)
            if s < 2:
                for j in range(16):
                    column = lane_gather(code, down + 8 * j)
                    place = down + (SLOTS + s * MOVE + g * 128 + 8 * j)
                    for later in range(s + 1, 3):
                        for f in range(4):
                            hit = jnp.where(column == leaving[later][f], place, 0)
                            key = (s, later, f)
                            found[key] = found[key] + hit if key in found else hit
        head = jnp.where(iota((16, MOVE), 0) == home[s : s + 1, :], 1.0, 0.0).astype(BF16)
        filled[s] = rows_dot(head, tail[s])
    for f in range(4):
        total = {key: jnp.sum(found[key + (f,)], axis=0, keepdims=True) for key in ((0, 1), (0, 2), (1, 2))}
        ptr[f : f + 1, :] = jnp.where(total[0, 1] > 0, total[0, 1], leaving[1][f])
        early = jnp.where(total[0, 2] > 0, total[0, 2], leaving[2][f])
        ptr[4 + f : 5 + f, :] = jnp.where(total[1, 2] > 0, total[1, 2], early)


def split(x):
    high = x.astype(BF16).astype(F32)
    return high, x - high


def step_kernel(
    counts, cells_h, slots_h, state, vel,
    pv_out, rows_out, dst,
    pool, rows, landed, block, faces, corners, halo_x, halo_y, halo_c, field, wx_table, sums, pv, out_pv, in_pv,
    cells, slots, home, tail, filled, ptr, first, later,
    local_sem, x_send, x_recv, y_send, y_recv, c_send, c_recv, r_send, r_recv, p_send, p_recv,
):
    me_x, me_y = lax.axis_index("gx"), lax.axis_index("gy")
    n_x, n_y = lax.axis_size("gx"), lax.axis_size("gy")

    def toward(r):
        dx, dy = OFFSETS[r]
        return (lax.rem(me_x + dx + n_x, n_x), lax.rem(me_y + dy + n_y, n_y))

    def remote(source, target, send, recv, r):
        return pltpu.make_async_remote_copy(
            src_ref=source, dst_ref=target, send_sem=send, recv_sem=recv,
            device_id=toward(r), device_id_type=pl.DeviceIdType.MESH,
        )

    load_vel = pltpu.make_async_copy(vel, block, local_sem.at[0])
    load_first = pltpu.make_async_copy(slots_h.at[:, pl.ds(0, MOVE)], first, local_sem.at[4])
    load_state = pltpu.make_async_copy(state, pool.at[pl.ds(0, SLOTS)], local_sem.at[1])
    load_slots = pltpu.make_async_copy(slots_h.at[:, pl.ds(0, MOVE)], slots, local_sem.at[5])
    load_cells = pltpu.make_async_copy(cells_h, cells, local_sem.at[6])
    for load in (load_vel, load_first, load_state, load_slots, load_cells):
        load.start()

    barrier = pltpu.get_barrier_semaphore()
    for r in range(8):
        pl.semaphore_signal(barrier, inc=1, device_id=toward(r), device_id_type=pl.DeviceIdType.MESH)
    load_vel.wait()
    faces[0] = edges(block, 0)
    faces[1] = edges(block, 15)
    for c in range(4):
        corners[c] = corner_rows(block, c)
    pl.semaphore_wait(barrier, 8)

    def rows_target(s, r):
        return landed.at[s, pl.ds((r ^ 1) * CAP, CAP)]

    def halo(s):
        part = pl.ds(s * 3, 3)
        copies = []
        for side, x, r in ((1, 0, 1), (0, 15, 0)):
            copies.append(remote(block.at[part, x], halo_x.at[side, part], x_send.at[s, side], x_recv.at[s, side], r))
        for side, edge, r in ((1, 0, 3), (0, 1, 2)):
            copies.append(remote(faces.at[edge, part], halo_y.at[side, part], y_send.at[s, side], y_recv.at[s, side], r))
        return copies

    corner_copies = [
        remote(corners.at[c], halo_c.at[3 - c], c_send.at[c], c_recv.at[3 - c], r)
        for c, r in ((0, 5), (1, 7), (2, 6), (3, 4))
    ]
    halos = [halo(s) for s in range(3)]
    row_copies = [
        [
            remote(rows.at[s, pl.ds(r * CAP, CAP)], rows_target(s, r), r_send.at[s, r], r_recv.at[s, r ^ 1], r)
            for r in range(8)
        ]
        for s in range(3)
    ]
    pv_copies = [
        [remote(out_pv.at[s, r // 2], in_pv.at[s, r ^ 1], p_send.at[s, r], p_recv.at[s, r ^ 1], r) for r in range(8)]
        for s in range(3)
    ]
    for copy in halos[0] + corner_copies:
        copy.start()
    load_first.wait()
    load_state.wait()
    copy_rows(rows.at[0], pool, lambda g, u: first[0, g * 128 + u])
    for copy in row_copies[0]:
        copy.start()
    for copy in halos[1] + halos[2]:
        copy.start()
    for b in range(16):
        pv[:, b * 128 : (b + 1) * 128] = pool[b * 128 : (b + 1) * 128, :].T[0:8, :]
    load_slots.wait()
    tables(counts, slots, ptr, dst, home, tail, filled)
    load_later = pltpu.make_async_copy(ptr, later, local_sem.at[7])
    load_later.start()
    for s in range(3):
        for k in range(3):
            own = block[s * 3 + k].reshape(256, 128)
            field[s, k * 256 : (k + 1) * 256, 0:128] = own
            field[s, k * 256 : (k + 1) * 256, 128:256] = own
    load_cells.wait()
    load_later.wait()

    def both(target, value):
        target[:, 0:128] = value
        target[:, 128:256] = value

    def place_halo(s):
        for copy in halos[s]:
            copy.wait_recv()
        for side in range(2):
            both(field.at[s, pl.ds(768 + side * 48, 48)], halo_x[side, s * 3 : s * 3 + 3].reshape(48, 128))
            both(field.at[s, pl.ds(864 + side * 48, 48)], halo_y[side, s * 3 : s * 3 + 3].reshape(48, 128))
        for c in range(4):
            both(field.at[s, pl.ds(960 + c * 16, 16)], halo_c[c])

    def interpolate(s):
        def chunk(i, carry):
            at = pl.ds(pl.multiple_of(i * CHUNK, CHUNK), CHUNK)
            fx, fy, fz = pv[0:1, at], pv[1:2, at], pv[2:3, at]
            cx, cy, cz = cells[s, 0:1, at], cells[s, 1:2, at], cells[s, 2:3, at]
            near_hi, near_lo = split(1.0 - fz)
            far_hi, far_lo = split(fz)
            level = iota((128, CHUNK), 0)
            near = level == cz
            far = level == cz + 1
            weight = jnp.concatenate(
                [
                    jnp.where(near, near_hi, jnp.where(far, far_hi, 0.0)).astype(BF16),
                    jnp.where(near, near_lo, jnp.where(far, far_lo, 0.0)).astype(BF16),
                ],
                axis=0,
            )
            sums[...] = jnp.dot(field[s], weight, preferred_element_type=F32)
            spot = iota((16, CHUNK), 0)
            wx = jnp.where(spot == cx, 1.0 - fx, jnp.where(spot == cx + 1, fx, 0.0))
            wy = jnp.where(spot == cy, 1.0 - fy, jnp.where(spot == cy + 1, fy, 0.0))
            wx_table[...] = wx
            wx_low = jnp.where(cx == -1, 1.0 - fx, 0.0)
            wx_high = jnp.where(cx == 15, fx, 0.0)
            wy_low = jnp.where(cy == -1, 1.0 - fy, 0.0)
            wy_high = jnp.where(cy == 15, fy, 0.0)
            corner = jnp.zeros((16, CHUNK), F32)
            for c, w in enumerate((wx_low * wy_low, wx_low * wy_high, wx_high * wy_low, wx_high * wy_high)):
                corner = corner + sums[960 + c * 16 : 976 + c * 16, :] * w
            old = pv[:, at]
            new = []
            speeds = []
            for k in range(3):
                along = sums[768 + k * 16 : 784 + k * 16, :] * wx_low + sums[816 + k * 16 : 832 + k * 16, :] * wx_high
                for x in range(16):
                    along = along + sums[k * 256 + x * 16 : k * 256 + x * 16 + 16, :] * wx_table[x : x + 1, :]
                edge = sums[864 + k * 16 : 880 + k * 16, :] * wy_low + sums[912 + k * 16 : 928 + k * 16, :] * wy_high
                total = along * wy + edge * wx + jnp.where(spot == s * 3 + k, corner, 0.0)
                speed = jnp.sum(total, axis=0, keepdims=True)
                speeds.append(speed)
                new.append(old[k : k + 1] + GAMMA[s] * speed + ZETA[s] * old[3 + k : 4 + k])
            for k in range(3):
                pv[k : k + 1, at] = new[k]
                pv[3 + k : 4 + k, at] = speeds[k]
            return carry

        lax.fori_loop(0, SLOTS // CHUNK, chunk, 0)

    def collect(s):
        for g in range(4):
            q = slots[s : s + 1, g * 128 : (g + 1) * 128]
            low = jnp.broadcast_to(q & 127, (8, 128))
            high = jnp.broadcast_to(q >> 7, (8, 128))
            picked = jnp.zeros((8, 128), F32)
            for h in range(16):
                picked = jnp.where(high == h, lane_gather(pv[:, h * 128 : (h + 1) * 128], low), picked)
            out_pv[s, g] = picked

    def deliver(s):
        lane = iota((8, 128), 1)
        came = [jnp.where(lane < CAP, in_pv[s, 2 * g + 1], in_pv[s, 2 * g]) for g in range(4)]
        value = jnp.concatenate(came, axis=1)
        high, rest = split(value)
        middle, low = split(rest)
        to = home[s : s + 1, :]
        parts = [jnp.where(to == h, part, 0.0).astype(BF16) for part in (high, middle, low) for h in range(16)]
        spread = rows_dot(jnp.concatenate(parts, axis=0), tail[s])
        for h in range(16):
            at = slice(h * 128, (h + 1) * 128)
            r = h * 8
            new = spread[r : r + 8] + spread[128 + r : 136 + r] + spread[256 + r : 264 + r]
            pv[:, at] = jnp.where(filled[s, h : h + 1, :] > 0.5, new, pv[:, at])

    for copy in corner_copies:
        copy.wait_recv()
    stores = []
    for s in range(3):
        place_halo(s)
        interpolate(s)
        collect(s)
        for copy in pv_copies[s]:
            copy.start()
        for copy in row_copies[s]:
            copy.wait_recv()
        store = pltpu.make_async_copy(landed.at[s], rows_out.at[pl.ds(s * MOVE, MOVE)], local_sem.at[8 + s])
        store.start()
        stores.append(store)
        if s < 2:
            pool[SLOTS + s * MOVE : SLOTS + (s + 1) * MOVE, :] = landed[s]
            copy_rows(rows.at[s + 1], pool, lambda g, u: later[s * 4 + g, u])
            for copy in row_copies[s + 1]:
                copy.start()
        for copy in pv_copies[s]:
            copy.wait_recv()
        deliver(s)
    pv_out[...] = pv[...]
    for store in stores:
        store.wait()
    for copies in halos + [corner_copies] + row_copies + pv_copies:
        for copy in copies:
            copy.wait_send()


def finish_kernel(dst_h, state, rows_h, pv_h, out, held, rows, pv, dst, sem, out_sem):
    loads = [
        pltpu.make_async_copy(state, held.at[pl.ds(0, SLOTS)], sem.at[0]),
        pltpu.make_async_copy(dst_h, dst, sem.at[1]),
        pltpu.make_async_copy(rows_h, rows, sem.at[2]),
        pltpu.make_async_copy(pv_h, pv, sem.at[3]),
    ]
    for load in loads:
        load.start()
    for load in loads:
        load.wait()

    def body(g, carry):
        for u in range(128):
            held[pl.ds(dst[g, u], 1), :] = rows[pl.ds(g * 128 + u, 1), :]
        return carry

    lax.fori_loop(0, 12, body, 0)
    stores = []
    for c in range(4):
        for b in range(c * 4, c * 4 + 4):
            held[b * 128 : (b + 1) * 128, 0:8] = pv[:, b * 128 : (b + 1) * 128].T
        part = pl.ds(c * 512, 512)
        stores.append(pltpu.make_async_copy(held.at[part], out.at[part], out_sem.at[c]))
        stores[-1].start()
    for store in stores:
        store.wait()


def whole(space):
    return pl.BlockSpec(memory_space=space)


def shape(dims, dtype):
    return jax.ShapeDtypeStruct(dims, dtype)


def local(state, velocity, cells, slots, counts):
    dma = pltpu.SemaphoreType.DMA
    pv, rows, dst = pl.pallas_call(
        step_kernel,
        out_shape=(shape((8, SLOTS), F32), shape((3 * MOVE, 128), F32), shape((12, 128), I32)),
        in_specs=[whole(SMEM)] + [whole(ANY)] * 4,
        out_specs=[whole(VMEM), whole(ANY), whole(VMEM)],
        scratch_shapes=[
            VMEM((SLOTS + 2 * MOVE, 128), F32),
            VMEM((3, MOVE, 128), F32),
            VMEM((3, MOVE, 128), F32),
            VMEM((9, 16, 16, 128), BF16),
            VMEM((2, 9, 16, 128), BF16),
            VMEM((4, 16, 128), BF16),
            VMEM((2, 9, 16, 128), BF16),
            VMEM((2, 9, 16, 128), BF16),
            VMEM((4, 16, 128), BF16),
            VMEM((3, 1024, 256), BF16),
            VMEM((16, CHUNK), F32),
            VMEM((1024, CHUNK), F32),
            VMEM((8, SLOTS), F32),
            VMEM((3, 4, 8, 128), F32),
            VMEM((3, 8, 8, 128), F32),
            VMEM((3, 3, SLOTS), I32),
            VMEM((3, MOVE), I32),
            VMEM((3, MOVE), I32),
            VMEM((3, 128, MOVE), BF16),
            VMEM((3, 16, 128), F32),
            VMEM((8, 128), I32),
            SMEM((3, MOVE), I32),
            SMEM((8, 128), I32),
            dma((11,)),
            dma((3, 2)), dma((3, 2)), dma((3, 2)), dma((3, 2)),
            dma((4,)), dma((4,)),
            dma((3, 8)), dma((3, 8)), dma((3, 8)), dma((3, 8)),
        ],
        compiler_params=pltpu.CompilerParams(collective_id=0, has_side_effects=True),
        name="step",
    )(counts, cells, slots, state, velocity.reshape(9, 16, 16, 128))

    return pl.pallas_call(
        finish_kernel,
        out_shape=shape((SLOTS, 128), F32),
        in_specs=[whole(ANY)] * 4,
        out_specs=whole(ANY),
        scratch_shapes=[
            VMEM((SLOTS + 8, 128), F32),
            VMEM((3 * MOVE, 128), F32),
            VMEM((8, SLOTS), F32),
            SMEM((12, 128), I32),
            dma((4,)),
            dma((4,)),
        ],
        name="finish",
    )(dst, state, rows, pv)


def solution(mesh):
    return jax.shard_map(
        local,
        mesh=mesh,
        in_specs=(
            P(("gx", "gy"), None),
            P(None, None, "gx", "gy", None),
            P(None, None, ("gx", "gy")),
            P(None, ("gx", "gy")),
            P(None, "gx", "gy", None),
        ),
        out_specs=P(("gx", "gy"), None),
        check_vma=False,
    )
```

time: 68.3 us -> 57.7 us (0.84)
  Pallas kernels: 64.7 us -> 57.5 us
  local copies, waits for them, and re-layouts: 3.25 us -> 0 us
    pallas_call x1 -> x0, Pallas kernels: 3.78 us -> none  [local(): pl.pallas_call(prep_kernel, grid=(1,), out_shape=(shape((8, SLOTS), F32),...]
    pallas_call x1, Pallas kernels: 7.19 us -> 3.88 us  [local(): pl.pallas_call(finish_kernel, out_shape=shape((SLOTS, 128), F32), in_spec...]
    unnamed x9 -> x0, local copies, waits for them, and re-layouts: 3.25 us -> none
where the time goes in v1:
time: 57.7 us; the launch traced here: 57.5 us
  Pallas kernels  57.5 us (100%)
    pallas_call x1, Pallas kernels, local(): pl.pallas_call(step_kernel, out_shape=(shape((8, SLOTS), F32), shape((3 *...  53.6 us
    pallas_call x1, Pallas kernels, local(): pl.pallas_call(finish_kernel, out_shape=shape((SLOTS, 128), F32), in_spec...  3.88 us

profile of v1, /device:TPU:1, one launch (start us, length us, event | category | flops | bytes accessed | tf_op | source)
XLA Modules:
  0.0 57.5 jit_solution(18097102550036597754)
XLA Ops:
  0.0 53.6 %step.1 = (f32[8,2048]{1,0:T(8,128)}, f32[1536,128]{1,0:T(8,128)}, s32[12,128]{1,0:T(8,128)}) custom-call(s32[3,1,1,8]{3,2,1,0:T(1,128)} %counts.1, s32[3,3,2048]{2,1,0:T(4,128)} %cells_h.1, s32[3,2048]{1,0:T(4,128)} %slots_h.1, f32[2048,128]{1,0:T(8,128)} %state.3, bf16[9,16,16,128]{3,2,1,0:T(8,128)(2,1)} %bitcast.1), custom_call_target="tpu_custom_call" | custom-call | tf_op jit(solution)/shard_map/step/pallas_call | solution.py:340
  53.6 3.9 %finish.1 = f32[2048,128]{1,0:T(8,128)} custom-call(s32[12,128]{1,0:T(8,128)} %get-tuple-element.8.dst_h, f32[2048,128]{1,0:T(8,128)} %state.3, f32[1536,128]{1,0:T(8,128)} %get-tuple-element.9.rows_h, f32[8,2048]{1,0:T(8,128)} %get-tuple-element.10.pv_h), custom_call_target="tpu_custom_call" | custom-call | tf_op jit(solution)/shard_map/finish/pallas_call | solution.py:378

commit v2 on v1

--- a/solution.py
+++ b/solution.py
@@ -28,13 +28,16 @@
     return jnp.take_along_axis(x, index, axis=1, mode="promise_in_bounds")
 
 
-def copy_rows(target, source, index):
+def copy_rows(target, source, index, copies):
     def body(g, carry):
         for u in range(128):
             target[pl.ds(g * 128 + u, 1), :] = source[pl.ds(index(g, u), 1), :]
         return carry
 
-    lax.fori_loop(0, MOVE // 128, body, 0)
+    for half in range(2):
+        lax.fori_loop(half * 2, half * 2 + 2, body, 0)
+        for r in range(half * 4, half * 4 + 4):
+            copies[r].start()
 
 
 def edges(block, y):
@@ -97,7 +100,7 @@
     counts, cells_h, slots_h, state, vel,
     pv_out, rows_out, dst,
     pool, rows, landed, block, faces, corners, halo_x, halo_y, halo_c, field, wx_table, sums, pv, out_pv, in_pv,
-    cells, slots, home, tail, filled, ptr, first, later,
+    cells, away, slots, home, tail, filled, ptr, first, later,
     local_sem, x_send, x_recv, y_send, y_recv, c_send, c_recv, r_send, r_recv, p_send, p_recv,
 ):
     me_x, me_y = lax.axis_index("gx"), lax.axis_index("gy")
@@ -163,9 +166,7 @@
         copy.start()
     load_first.wait()
     load_state.wait()
-    copy_rows(rows.at[0], pool, lambda g, u: first[0, g * 128 + u])
-    for copy in row_copies[0]:
-        copy.start()
+    copy_rows(rows.at[0], pool, lambda g, u: first[0, g * 128 + u], row_copies[0])
     for copy in halos[1] + halos[2]:
         copy.start()
     for b in range(16):
@@ -195,63 +196,89 @@
         for c in range(4):
             both(field.at[s, pl.ds(960 + c * 16, 16)], halo_c[c])
 
+    def advance(s, part, table, old, cell):
+        fx, fy, fz = old[0:1], old[1:2], old[2:3]
+        cx, cy, cz = cell
+        near_hi, near_lo = split(1.0 - fz)
+        far_hi, far_lo = split(fz)
+        level = iota((128, CHUNK), 0)
+        near = level == cz
+        far = level == cz + 1
+        weight = jnp.concatenate(
+            [
+                jnp.where(near, near_hi, jnp.where(far, far_hi, 0.0)).astype(BF16),
+                jnp.where(near, near_lo, jnp.where(far, far_lo, 0.0)).astype(BF16),
+            ],
+            axis=0,
+        )
+        part[...] = jnp.dot(field[s], weight, preferred_element_type=F32)
+        spot = iota((16, CHUNK), 0)
+        wx = jnp.where(spot == cx, 1.0 - fx, jnp.where(spot == cx + 1, fx, 0.0))
+        wy = jnp.where(spot == cy, 1.0 - fy, jnp.where(spot == cy + 1, fy, 0.0))
+        table[...] = wx
+        wx_low = jnp.where(cx == -1, 1.0 - fx, 0.0)
+        wx_high = jnp.where(cx == 15, fx, 0.0)
+        wy_low = jnp.where(cy == -1, 1.0 - fy, 0.0)
+        wy_high = jnp.where(cy == 15, fy, 0.0)
+        corner = jnp.zeros((16, CHUNK), F32)
+        for c, w in enumerate((wx_low * wy_low, wx_low * wy_high, wx_high * wy_low, wx_high * wy_high)):
+            corner = corner + part[960 + c * 16 : 976 + c * 16, :] * w
+        new = []
+        speeds = []
+        for k in range(3):
+            along = part[768 + k * 16 : 784 + k * 16, :] * wx_low + part[816 + k * 16 : 832 + k * 16, :] * wx_high
+            for x in range(16):
+                along = along + part[k * 256 + x * 16 : k * 256 + x * 16 + 16, :] * table[x : x + 1, :]
+            edge = part[864 + k * 16 : 880 + k * 16, :] * wy_low + part[912 + k * 16 : 928 + k * 16, :] * wy_high
+            total = along * wy + edge * wx + jnp.where(spot == s * 3 + k, corner, 0.0)
+            speed = jnp.sum(total, axis=0, keepdims=True)
+            speeds.append(speed)
+            new.append(old[k : k + 1] + GAMMA[s] * speed + ZETA[s] * old[3 + k : 4 + k])
+        return new + speeds
+
     def interpolate(s):
         def chunk(i, carry):
             at = pl.ds(pl.multiple_of(i * CHUNK, CHUNK), CHUNK)
-            fx, fy, fz = pv[0:1, at], pv[1:2, at], pv[2:3, at]
-            cx, cy, cz = cells[s, 0:1, at], cells[s, 1:2, at], cells[s, 2:3, at]
-            near_hi, near_lo = split(1.0 - fz)
-            far_hi, far_lo = split(fz)
-            level = iota((128, CHUNK), 0)
-            near = level == cz
-            far = level == cz + 1
-            weight = jnp.concatenate(
-                [
-                    jnp.where(near, near_hi, jnp.where(far, far_hi, 0.0)).astype(BF16),
-                    jnp.where(near, near_lo, jnp.where(far, far_lo, 0.0)).astype(BF16),
-                ],
-                axis=0,
-            )
-            sums[...] = jnp.dot(field[s], weight, preferred_element_type=F32)
-            spot = iota((16, CHUNK), 0)
-            wx = jnp.where(spot == cx, 1.0 - fx, jnp.where(spot == cx + 1, fx, 0.0))
-            wy = jnp.where(spot == cy, 1.0 - fy, jnp.where(spot == cy + 1, fy, 0.0))
-            wx_table[...] = wx
-            wx_low = jnp.where(cx == -1, 1.0 - fx, 0.0)
-            wx_high = jnp.where(cx == 15, fx, 0.0)
-            wy_low = jnp.where(cy == -1, 1.0 - fy, 0.0)
-            wy_high = jnp.where(cy == 15, fy, 0.0)
-            corner = jnp.zeros((16, CHUNK), F32)
-            for c, w in enumerate((wx_low * wy_low, wx_low * wy_high, wx_high * wy_low, wx_high * wy_high)):
-                corner = corner + sums[960 + c * 16 : 976 + c * 16, :] * w
-            old = pv[:, at]
-            new = []
-            speeds = []
-            for k in range(3):
-                along = sums[768 + k * 16 : 784 + k * 16, :] * wx_low + sums[816 + k * 16 : 832 + k * 16, :] * wx_high
-                for x in range(16):
-                    along = along + sums[k * 256 + x * 16 : k * 256 + x * 16 + 16, :] * wx_table[x : x + 1, :]
-                edge = sums[864 + k * 16 : 880 + k * 16, :] * wy_low + sums[912 + k * 16 : 928 + k * 16, :] * wy_high
-                total = along * wy + edge * wx + jnp.where(spot == s * 3 + k, corner, 0.0)
-                speed = jnp.sum(total, axis=0, keepdims=True)
-                speeds.append(speed)
-                new.append(old[k : k + 1] + GAMMA[s] * speed + ZETA[s] * old[3 + k : 4 + k])
-            for k in range(3):
-                pv[k : k + 1, at] = new[k]
-                pv[3 + k : 4 + k, at] = speeds[k]
+            cell = [cells[s, c : c + 1, at] for c in range(3)]
+            for k, value in enumerate(advance(s, sums.at[0], wx_table.at[0], pv[:, at], cell)):
+                pv[k : k + 1, at] = value
             return carry
 
         lax.fori_loop(0, SLOTS // CHUNK, chunk, 0)
 
-    def collect(s):
+    def pick(s, take, zero):
+        picked = []
         for g in range(4):
             q = slots[s : s + 1, g * 128 : (g + 1) * 128]
             low = jnp.broadcast_to(q & 127, (8, 128))
             high = jnp.broadcast_to(q >> 7, (8, 128))
-            picked = jnp.zeros((8, 128), F32)
+            value = zero
             for h in range(16):
-                picked = jnp.where(high == h, lane_gather(pv[:, h * 128 : (h + 1) * 128], low), picked)
-            out_pv[s, g] = picked
+                value = jnp.where(high == h, lane_gather(take(slice(h * 128, (h + 1) * 128)), low), value)
+            picked.append(value)
+        return picked
+
+    def collect_cells(s):
+        def packed(at):
+            one = (cells[s, 0:1, at] + 1) * 4096 + (cells[s, 1:2, at] + 1) * 128 + cells[s, 2:3, at]
+            return jnp.broadcast_to(one, (8, 128))
+
+        for g, value in enumerate(pick(s, packed, jnp.zeros((8, 128), I32))):
+            one = value[0:1]
+            at = slice(g * 128, (g + 1) * 128)
+            away[s, 0:1, at] = (one >> 12) - 1
+            away[s, 1:2, at] = ((one >> 7) & 31) - 1
+            away[s, 2:3, at] = one & 127
+
+    def collect(s):
+        old = jnp.concatenate(pick(s, lambda at: pv[:, at], jnp.zeros((8, 128), F32)), axis=1)
+        cell = [away[s, c : c + 1, :] for c in range(3)]
+        new = advance(s, sums.at[1], wx_table.at[1], old, cell)
+        for g in range(4):
+            at = slice(g * 128, (g + 1) * 128)
+            out_pv[s, g] = old[:, at]
+            for k in range(6):
+                out_pv[s, g, k : k + 1, :] = new[k][:, at]
 
     def deliver(s):
         lane = iota((8, 128), 1)
@@ -268,15 +295,17 @@
             new = spread[r : r + 8] + spread[128 + r : 136 + r] + spread[256 + r : 264 + r]
             pv[:, at] = jnp.where(filled[s, h : h + 1, :] > 0.5, new, pv[:, at])
 
+    for s in range(3):
+        collect_cells(s)
     for copy in corner_copies:
         copy.wait_recv()
     stores = []
     for s in range(3):
         place_halo(s)
-        interpolate(s)
         collect(s)
         for copy in pv_copies[s]:
             copy.start()
+        interpolate(s)
         for copy in row_copies[s]:
             copy.wait_recv()
         store = pltpu.make_async_copy(landed.at[s], rows_out.at[pl.ds(s * MOVE, MOVE)], local_sem.at[8 + s])
@@ -284,9 +313,7 @@
         stores.append(store)
         if s < 2:
             pool[SLOTS + s * MOVE : SLOTS + (s + 1) * MOVE, :] = landed[s]
-            copy_rows(rows.at[s + 1], pool, lambda g, u: later[s * 4 + g, u])
-            for copy in row_copies[s + 1]:
-                copy.start()
+            copy_rows(rows.at[s + 1], pool, lambda g, u: later[s * 4 + g, u], row_copies[s + 1])
         for copy in pv_copies[s]:
             copy.wait_recv()
         deliver(s)
@@ -353,12 +380,13 @@
             VMEM((2, 9, 16, 128), BF16),
             VMEM((4, 16, 128), BF16),
             VMEM((3, 1024, 256), BF16),
-            VMEM((16, CHUNK), F32),
-            VMEM((1024, CHUNK), F32),
+            VMEM((2, 16, CHUNK), F32),
+            VMEM((2, 1024, CHUNK), F32),
             VMEM((8, SLOTS), F32),
             VMEM((3, 4, 8, 128), F32),
             VMEM((3, 8, 8, 128), F32),
             VMEM((3, 3, SLOTS), I32),
+            VMEM((3, 8, MOVE), I32),
             VMEM((3, MOVE), I32),
             VMEM((3, MOVE), I32),
             VMEM((3, 128, MOVE), BF16),

time: 57.7 us -> 51.8 us (0.90)
  Pallas kernels: 57.5 us -> 51.6 us
    pallas_call x1, Pallas kernels: 53.6 us -> 47.7 us  [local(): pl.pallas_call(step_kernel, out_shape=(shape((8, SLOTS), F32), shape((3 *...]
where the time goes in v2:
time: 51.8 us; the launch traced here: 51.6 us
  Pallas kernels  51.6 us (100%)
    pallas_call x1, Pallas kernels, local(): pl.pallas_call(step_kernel, out_shape=(shape((8, SLOTS), F32), shape((3 *...  47.7 us
    pallas_call x1, Pallas kernels, local(): pl.pallas_call(finish_kernel, out_shape=shape((SLOTS, 128), F32), in_spec...  3.88 us

profile of v2, /device:TPU:1, one launch (start us, length us, event | category | flops | bytes accessed | tf_op | source)
XLA Modules:
  0.0 51.6 jit_solution(272723327427851773)
XLA Ops:
  0.0 47.7 %step.1 = (f32[8,2048]{1,0:T(8,128)}, f32[1536,128]{1,0:T(8,128)}, s32[12,128]{1,0:T(8,128)}) custom-call(s32[3,1,1,8]{3,2,1,0:T(1,128)} %counts.1, s32[3,3,2048]{2,1,0:T(4,128)} %cells_h.1, s32[3,2048]{1,0:T(4,128)} %slots_h.1, f32[2048,128]{1,0:T(8,128)} %state.3, bf16[9,16,16,128]{3,2,1,0:T(8,128)(2,1)} %bitcast.1), custom_call_target="tpu_custom_call" | custom-call | tf_op jit(solution)/shard_map/step/pallas_call | solution.py:367
  47.7 3.9 %finish.1 = f32[2048,128]{1,0:T(8,128)} custom-call(s32[12,128]{1,0:T(8,128)} %get-tuple-element.8.dst_h, f32[2048,128]{1,0:T(8,128)} %state.3, f32[1536,128]{1,0:T(8,128)} %get-tuple-element.9.rows_h, f32[8,2048]{1,0:T(8,128)} %get-tuple-element.10.pv_h), custom_call_target="tpu_custom_call" | custom-call | tf_op jit(solution)/shard_map/finish/pallas_call | solution.py:406
